TPU v7x, 32 devices: a whole 2x2x4 slice. The times are simulated.
32 devices in a mesh: replica: 8 (over y, x, core), mp: 4 (over z).
Axes of the slice: x: 2, y: 2, z: 4, core: 2. Of those that a mesh axis runs over, the one named last changes fastest.
Arguments:
- pseudo_grad: bfloat16 [8, 2, 3072, 2048], P('replica', None, None, 'mp'), may hold values from -6 to 6
- outer_params: float32 [2, 3072, 2048], P(None, 'replica', 'mp'), may hold values from -6 to 6
- momentum: float32 [2, 3072, 2048], P(None, 'replica', 'mp'), may hold values from -3 to 3
- acts: bfloat16 [1024, 3072], P('replica', 'mp'), may hold values from -6 to 6
- queries: bfloat16 [1024, 2048], P('replica', 'mp'), may hold values from -6 to 6
- keys: bfloat16 [1024, 2048], P('replica', 'mp'), may hold values from -6 to 6
- doc_ids: int32 [1024], P('replica'), may hold values from 0 to 31, never falling along the last dimension, each value on 1 to 64 neighbouring positions
Outputs:
- new_outer: float32 [2, 3072, 2048], P(None, 'replica', 'mp')
- new_momentum: float32 [2, 3072, 2048], P(None, 'replica', 'mp')
- new_local: bfloat16 [8, 3072, 2048], P('replica', None, 'mp')
Inputs may be any that keep to these rules, and one draw needn't show every extreme that they name: doc_ids never fall along the rows; each document covers 1 to 64 positions.
All inputs are finite; a program needn't handle non-finite values.
Results may differ from a plain program's by a relative error of at most 0.0037.
The roundings to bfloat16 on the way count: a program that leaves them out, or rounds other values in their place, can miss the bound.
Values may be sent and summed in bfloat16 or wider, within the bound.
A program may use at most 64 MiB of HBM per device.

v0:
```python
import jax
import jax.numpy as jnp
from jax import lax
from jax.sharding import PartitionSpec as P

HD = 256
norm_eps = 1e-06
outer_rate = 0.7
outer_beta = 0.9
inner_rate = 0.1


def attend(query, key_rows, value_rows, doc_rows):
    count = query.shape[0]
    scores = jnp.einsum(
        "qhd,khd->hqk", query, key_rows, preferred_element_type=jnp.float32
    ) * query.shape[2] ** (-0.5)
    row_pos = lax.broadcasted_iota(jnp.int32, (count, count), 0)
    col_pos = lax.broadcasted_iota(jnp.int32, (count, count), 1)
    allowed = (row_pos >= col_pos) & (doc_rows[:, None] == doc_rows[None, :])
    scores = jnp.where(allowed[None], scores, -1e30)
    probs = jax.nn.softmax(scores, axis=-1).astype(jnp.bfloat16)
    context = jnp.einsum("hqk,khd->qhd", probs, value_rows, preferred_element_type=jnp.float32)
    return context.astype(jnp.bfloat16)


def outer_update(summed, params_rows, moment_rows, workers):
    delta = summed / workers
    moment_next = outer_beta * moment_rows + delta
    params_next = params_rows - outer_rate * (delta + outer_beta * moment_next)
    return (params_next, moment_next)


def shards(pseudo_grad, outer_params, momentum, acts, queries, keys, doc_ids):
    workers = lax.axis_size("replica")
    groups = lax.axis_size("mp")
    full_x = lax.all_gather(acts, "mp", axis=1, tiled=True)
    blocks = lax.all_to_all(pseudo_grad, "replica", split_axis=2, concat_axis=0, tiled=True)
    summed = jnp.sum(blocks.astype(jnp.float32), axis=0)
    new_outer, new_momentum = outer_update(summed, outer_params, momentum, workers)
    weights = lax.all_gather(new_outer.astype(jnp.bfloat16), "replica", axis=1, tiled=True)
    count, width = full_x.shape
    cols = weights.shape[2]
    heads_here = cols // HD
    all_cols = cols * groups
    rows_f = full_x.astype(jnp.float32)
    normed = (
        rows_f * lax.rsqrt(jnp.mean(rows_f * rows_f, axis=-1, keepdims=True) + norm_eps)
    ).astype(jnp.bfloat16)
    values = (
        jnp.dot(normed, weights[0], preferred_element_type=jnp.float32) * width ** (-0.5)
    ).astype(jnp.bfloat16)
    query = queries.reshape(count, heads_here, HD)
    keyed = keys.reshape(count, heads_here, HD)

    def attn_fn(c):
        return attend(query, keyed, c, doc_ids)

    context, pullback = jax.vjp(attn_fn, values.reshape(count, heads_here, HD))
    ctx = context.reshape(count, cols)
    partial_branch = lax.dot_general(
        ctx, weights[1], (((1,), (1,)), ((), ())), preferred_element_type=jnp.float32
    ) * all_cols ** (-0.5)
    branch = lax.psum(partial_branch.astype(jnp.bfloat16), "mp").astype(jnp.float32)
    dout = (rows_f + branch - jnp.roll(rows_f, -1, axis=0)).astype(jnp.bfloat16)
    dctx = (
        jnp.dot(dout, weights[1], preferred_element_type=jnp.float32) * all_cols ** (-0.5)
    ).astype(jnp.bfloat16)
    pulled = pullback(dctx.reshape(count, heads_here, HD))[0]
    grad = lax.dot_general(
        normed,
        pulled.reshape(count, cols),
        (((0,), (0,)), ((), ())),
        preferred_element_type=jnp.float32,
    ) * width ** (-0.5)
    squares = lax.psum(jnp.sum(grad * grad), "mp")
    rms = jnp.sqrt(squares / (width * all_cols) + norm_eps)
    new_local = (weights[0].astype(jnp.float32) - inner_rate * grad / rms).astype(jnp.bfloat16)
    return (new_outer, new_momentum, new_local[None])


def solution(mesh):
    placed = (
        P("replica", None, None, "mp"),
        P(None, "replica", "mp"),
        P(None, "replica", "mp"),
        P("replica", "mp"),
        P("replica", "mp"),
        P("replica", "mp"),
        P("replica"),
    )
    return jax.shard_map(
        shards,
        mesh=mesh,
        in_specs=placed,
        out_specs=(P(None, "replica", "mp"), P(None, "replica", "mp"), P("replica", None, "mp")),
        check_vma=False,
    )
```

profile of v0, /device:TPU:0, one launch (start us, length us, event | category | flops | bytes accessed | tf_op | source)
XLA Modules:
  0.0 232.5 jit_solution(10670747100160510871)
XLA Ops:
  7.2 0.0 all-gather.2.cloned.1.call-start
  7.2 11.1 %copy.23 = bf16[1,2,3072,512]{3,1,0,2:T(2,128)(2,1)S(1)} copy(bf16[1,2,3072,512]{3,2,1,0:T(8,128)(2,1)} %param.7) | data formatting | bytes 12582912 | tf_op args[0]
  18.3 76.5 %all_to_all.4 = bf16[1,2,3072,512]{3,1,0,2:T(2,128)(2,1)S(1)} all-to-all(bf16[1,2,3072,512]{3,1,0,2:T(2,128)(2,1)S(1)} %copy.23), channel_id=1, replica_groups=mesh['replica'=8,'mp'=4] {'replica'}, dimensions={2} | all-to-all | bytes 12582912 | tf_op jit(solution)/shard_map/all_to_all | solution.py:38
  94.8 0.0 copy-start
  94.8 0.0 copy-start.1
  94.8 6.3 %convert_reduce_fusion = f32[2,384,512]{2,0,1:T(2,128)S(1)} fusion(bf16[2,8,384,512]{3,0,2,1:T(2,128)(2,1)S(1)} %bitcast.46), kind=kLoop, calls=%fused_computation.1 | loop fusion | flops 5898240 | bytes 7864320 | tf_op jit(solution)/shard_map/reduce_sum | solution.py:39
  101.1 0.0 copy-done
  101.1 0.0 copy-done.1
  101.1 0.0 copy-start.3
  101.1 0.0 copy-start.4
  101.1 0.0 copy-start.5
  101.1 0.0 copy-start.2
  101.1 2.7 %fusion.21 = (bf16[2,384,512]{2,1,0:T(8,128)(2,1)}, f32[2,384,512]{2,1,0:T(8,128)}, f32[2,384,512]{2,1,0:T(8,128)}) fusion(f32[2,384,512]{2,1,0:T(8,128)S(1)} %copy-done, f32[2,384,512]{2,0,1:T(2,128)S(1)} %convert_reduce_fusion, f32[2,384,512]{2,1,0:T(8,128)S(1)} %copy-done.1), kind=kLoop, calls=%fused_computation.38 | loop fusion | flops 3145728 | bytes 8650752 | tf_op jit(solution)/shard_map/convert_element_type | solution.py:41
  103.8 0.0 all-gather.2.cloned.1.call-update
  103.8 0.0 all-reduce.2.cloned.1.call-start
  103.9 0.0 copy-done.3
  103.9 0.1 fusion.19
  104.0 0.0 copy-done.4
  104.0 0.0 copy-done.5
  104.0 0.2 fusion.12
  104.2 0.1 fusion.22
  104.3 0.0 copy-done.2
  104.3 19.8 %all_gather.7 = bf16[128,3072]{1,0:T(8,128)(2,1)S(1)} all-gather(bf16[128,768]{1,0:T(8,128)(2,1)S(1)} %copy-done.2), channel_id=1, replica_groups=mesh['replica'=8,'mp'=4] {'mp'}, dimensions={1}, use_global_device_ids=true | all-gather | bytes 983040 | tf_op jit(solution)/shard_map/all_gather | solution.py:37
  124.1 0.2 multiply_reduce_fusion.1
  124.3 24.4 %all-gather.2.cloned.1.call-done = bf16[2,3072,512]{2,1,0:T(8,128)(2,1)} async-done(((bf16[2,384,512]{2,1,0:T(8,128)(2,1)}), bf16[2,3072,512]{2,1,0:T(8,128)(2,1)}) %all-gather.2.cloned.1.call-update) | async-done | bytes 6291472 | tf_op jit(solution)/shard_map/all_gather | solution.py:41
  148.7 2.5 %fusion.9 = bf16[128,512]{1,0:T(8,128)(2,1)S(1)} fusion(bf16[2,3072,512]{2,1,0:T(8,128)(2,1)} %all-gather.2.cloned.1.call-done, bf16[128,3072]{1,0:T(8,128)(2,1)S(1)} %all_gather.7, f32[128]{0:T(128)S(1)} %add_rsqrt_fusion), kind=kOutput, calls=%fused_computation.23 | convolution fusion | flops 403963904 | bytes 4063744 | tf_op jit(solution)/shard_map/dot_general | solution.py:51
  151.3 0.1 copy.33
  151.4 0.2 convolution_convert_fusion.1
  151.6 3.9 %fusion.1 = bf16[128,3072]{1,0:T(8,128)(2,1)} fusion(bf16[128,512]{0,1:T(8,128)(2,1)S(1)} %bitcast.52, bf16[2,3072,512]{2,1,0:T(8,128)(2,1)} %all-gather.2.cloned.1.call-done), kind=kOutput, calls=%fused_computation.5 | convolution fusion | flops 403439616 | bytes 4063232 | tf_op jit(solution)/shard_map/dot_general | solution.py:61
  155.5 0.0 all-reduce.2.cloned.1.call-update
  155.6 0.2 slice.22
  155.8 43.8 %all-reduce.2.cloned.1.call-done = bf16[128,3072]{1,0:T(8,128)(2,1)} async-done(((bf16[128,3072]{1,0:T(8,128)(2,1)}), bf16[128,3072]{1,0:T(8,128)(2,1)}) %all-reduce.2.cloned.1.call-update) | async-done | bytes 786448 | tf_op jit(solution)/shard_map/psum | solution.py:64
  199.6 2.8 %fusion.10 = bf16[128,512]{1,0:T(8,128)(2,1)S(1)} fusion(bf16[2,3072,512]{2,1,0:T(8,128)(2,1)} %all-gather.2.cloned.1.call-done, f32[1,3072]{1,0:T(1,128)S(1)} %slice.23, f32[127,3072]{1,0:T(8,128)S(1)} %slice.22, bf16[128,3072]{1,0:T(8,128)(2,1)} %all-reduce.2.cloned.1.call-done, bf16[128,3072]{1,0:T(8,128)(2,1)S(1)} %all_gather.7), kind=kOutput, calls=%fused_computation.24 | convolution fusion | flops 405143552 | bytes 6422528 | tf_op jit(solution)/shard_map/dot_general | solution.py:67
  202.4 0.1 copy.34
  202.5 0.2 convolution_convert_fusion
  202.7 5.1 %multiply_reduce_fusion = (f32[]{:T(128)}, f32[3072,512]{1,0:T(8,128)}) fusion(bf16[128,512]{0,1:T(8,128)(2,1)S(1)} %bitcast.47, bf16[128,3072]{1,0:T(8,128)(2,1)S(1)} %all_gather.7, f32[128]{0:T(128)S(1)} %add_rsqrt_fusion), kind=kOutput, calls=%fused_computation.3 | convolution fusion | flops 408551424 | bytes 7209476 | tf_op jit(solution)/shard_map/dot_general | solution.py:70
  207.8 10.6 %psum.15 = f32[]{:T(128)} all-reduce(f32[]{:T(128)} %get-tuple-element.6), channel_id=1, replica_groups=mesh['replica'=8,'mp'=4] {'mp'}, use_global_device_ids=true, to_apply=%region_6.7 | all-reduce | flops 1 | bytes 8 | tf_op jit(solution)/shard_map/psum | solution.py:76
  219.1 6.5 %fusion.2 = bf16[1,3072,512]{2,1,0:T(8,128)(2,1)} fusion(f32[]{:T(128)S(6)} %sqrt.3, f32[3072,512]{1,0:T(8,128)} %get-tuple-element.7, bf16[2,3072,512]{2,1,0:T(8,128)(2,1)} %all-gather.2.cloned.1.call-done), kind=kLoop, calls=%fused_computation.8 | loop fusion | flops 7864320 | bytes 12582916 | tf_op jit(solution)/shard_map/broadcast_in_dim | solution.py:79
  (2 shorter events, 0.0 us)
Async XLA Ops:
  7.2 141.6 %all-gather.2.cloned.1.call-start = ((), (), s32[]{:S(2)}) async-start(), calls=%async_computation.1 | async-start | bytes 7077888 | tf_op jit(solution)/shard_map/all_gather | solution.py:41
  94.8 6.3 %copy-start = (f32[2,384,512]{2,1,0:T(8,128)S(1)}, f32[2,384,512]{2,1,0:T(8,128)}, u32[]{:S(2)}) copy-start(f32[2,384,512]{2,1,0:T(8,128)} %param.8) | copy-start | bytes 4718596
  94.8 6.3 %copy-start.1 = (f32[2,384,512]{2,1,0:T(8,128)S(1)}, f32[2,384,512]{2,1,0:T(8,128)}, u32[]{:S(2)}) copy-start(f32[2,384,512]{2,1,0:T(8,128)} %param.9) | copy-start | bytes 4718596
  101.1 2.8 %copy-start.3 = (s32[128]{0:T(128)S(1)}, s32[128]{0:T(128)}, u32[]{:S(2)}) copy-start(s32[128]{0:T(128)} %param.13) | copy-start | bytes 1540
  101.1 2.9 %copy-start.4 = (bf16[128,512]{1,0:T(8,128)(2,1)S(1)}, bf16[128,512]{1,0:T(8,128)(2,1)}, u32[]{:S(2)}) copy-start(bf16[128,512]{1,0:T(8,128)(2,1)} %param.12) | copy-start | bytes 393220
  101.1 2.9 %copy-start.5 = (bf16[128,512]{1,0:T(8,128)(2,1)S(1)}, bf16[128,512]{1,0:T(8,128)(2,1)}, u32[]{:S(2)}) copy-start(bf16[128,512]{1,0:T(8,128)(2,1)} %param.11) | copy-start | bytes 393220
  101.1 3.1 %copy-start.2 = (bf16[128,768]{1,0:T(8,128)(2,1)S(1)}, bf16[128,768]{1,0:T(8,128)(2,1)}, u32[]{:S(2)}) copy-start(bf16[128,768]{1,0:T(8,128)(2,1)} %param.10) | copy-start | bytes 589828
  103.8 95.7 %all-reduce.2.cloned.1.call-start = ((), (), s32[]{:S(2)}) async-start(), calls=%async_computation.2 | async-start | bytes 1572864 | tf_op jit(solution)/shard_map/psum | solution.py:64
Sparse Core Ops, SparseCore 0:
  103.9 44.7 all-gather.1
  155.7 43.8 all-reduce.1
where the time goes:
time: 233 us; the launch traced here: 232 us
  blocking collectives  107 us (46%)
  waiting for transfers between devices  68.2 us (29%)
  other arithmetic  15.8 us (7%)
  matrix products  15 us (6%)
  between operations  14.9 us (6%)
  local copies, waits for them, and re-layouts  11.6 us (5%)
    all_to_all x1, blocking collectives, shards(): lax.all_to_all(pseudo_grad, 'replica', split_axis=2, concat_axis=0, tiled...  76.5 us
    psum x1, waiting for transfers between devices, shards(): lax.psum(partial_branch.astype(jnp.bfloat16), 'mp').astype(jnp.float32)  43.8 us
    all_gather x1, waiting for transfers between devices, shards(): lax.all_gather(new_outer.astype(jnp.bfloat16), 'replica', axis=1, tiled=T...  24.4 us
    all_gather x1, blocking collectives, shards(): full_x = lax.all_gather(acts, 'mp', axis=1, tiled=True)  19.8 us
    unnamed x13, local copies, waits for them, and re-layouts  11.1 us
    psum x1, blocking collectives, shards(): squares = lax.psum(jnp.sum(grad * grad), 'mp')  10.6 us
    broadcast_in_dim x1, other arithmetic, shards(): return (new_outer, new_momentum, new_local[None])  6.48 us
    reduce_sum x1, other arithmetic, shards(): summed = jnp.sum(blocks.astype(jnp.float32), axis=0)  6.26 us
  transfers between devices with their start and end apart: 2, of which 2 were waited for; matrix products, arithmetic and copies ran while one was open for 0% of the time, Pallas kernels for 0%

commit v1 on v0

--- a/solution.py
+++ b/solution.py
@@ -34,7 +34,8 @@
 def shards(pseudo_grad, outer_params, momentum, acts, queries, keys, doc_ids):
     workers = lax.axis_size("replica")
     groups = lax.axis_size("mp")
-    full_x = lax.all_gather(acts, "mp", axis=1, tiled=True)
+    pieces = lax.all_gather(acts, "mp")
+    full_x = jnp.concatenate(pieces, axis=1)
     blocks = lax.all_to_all(pseudo_grad, "replica", split_axis=2, concat_axis=0, tiled=True)
     summed = jnp.sum(blocks.astype(jnp.float32), axis=0)
     new_outer, new_momentum = outer_update(summed, outer_params, momentum, workers)

time: 233 us -> 234 us (level)
  local copies, waits for them, and re-layouts: 11.6 us -> 20.9 us
  waiting for transfers between devices: 68.2 us -> 59.1 us
    psum x1, waiting for transfers between devices: 43.8 us -> 35.6 us  [shards(): lax.psum(partial_branch.astype(jnp.bfloat16), 'mp').astype(jnp.float32)]
    convert_element_type x0 -> x3, local copies, waits for them, and re-layouts: none -> 5.21 us  [the longest x2 4.84 us: shards(): rows_f = full_x.astype(jnp.float32)]
    slice x2 -> x4, local copies, waits for them, and re-layouts: 0.21 us -> 3.44 us  [shards(): dout = (rows_f + branch - jnp.roll(rows_f, -1, axis=0)).astype(jnp.bfloat16)]
    unnamed x13 -> x21, local copies, waits for them, and re-layouts: 11.1 us -> 12 us
  transfers between devices with their start and end apart: 2 -> 2, of which waited for: 2 -> 2; matrix products, arithmetic and copies ran while one was open for 0% -> 4% of each run, Pallas kernels for 0% -> 0%
where the time goes in v1:
time: 234 us
  blocking collectives  107 us (46%)
  waiting for transfers between devices  59.1 us (25%)
  local copies, waits for them, and re-layouts  20.9 us (9%)
  other arithmetic  16.2 us (7%)
  matrix products  15.2 us (6%)
  between operations  14.9 us (6%)
    all_to_all x1, blocking collectives, shards(): lax.all_to_all(pseudo_grad, 'replica', split_axis=2, concat_axis=0, tiled...  76.5 us
    psum x1, waiting for transfers between devices, shards(): lax.psum(partial_branch.astype(jnp.bfloat16), 'mp').astype(jnp.float32)  35.6 us
    all_gather x1, waiting for transfers between devices, shards(): lax.all_gather(new_outer.astype(jnp.bfloat16), 'replica', axis=1, tiled=T...  23.5 us
    all_gather x1, blocking collectives, shards(): pieces = lax.all_gather(acts, 'mp')  19.8 us
    unnamed x21, local copies, waits for them, and re-layouts  12 us
    psum x1, blocking collectives, shards(): squares = lax.psum(jnp.sum(grad * grad), 'mp')  10.6 us
    broadcast_in_dim x1, other arithmetic, shards(): return (new_outer, new_momentum, new_local[None])  6.48 us
    reduce_sum x1, other arithmetic, shards(): summed = jnp.sum(blocks.astype(jnp.float32), axis=0)  6.26 us
  transfers between devices with their start and end apart: 2, of which 2 were waited for; matrix products, arithmetic and copies ran while one was open for 4% of the time, Pallas kernels for 0%

profile of v1, /device:TPU:0, one launch (start us, length us, event | category | flops | bytes accessed | tf_op | source)
XLA Modules:
  0.0 233.5 jit_solution(5605690547960112061)
XLA Ops:
  7.2 0.0 all-gather.3.cloned.1.call-start
  7.2 11.1 %copy.46 = bf16[1,2,3072,512]{3,1,0,2:T(2,128)(2,1)S(1)} copy(bf16[1,2,3072,512]{3,2,1,0:T(8,128)(2,1)} %param.7) | data formatting | bytes 12582912 | tf_op args[0]
  18.3 76.5 %all_to_all.4 = bf16[1,2,3072,512]{3,1,0,2:T(2,128)(2,1)S(1)} all-to-all(bf16[1,2,3072,512]{3,1,0,2:T(2,128)(2,1)S(1)} %copy.46), channel_id=1, replica_groups=mesh['replica'=8,'mp'=4] {'replica'}, dimensions={2} | all-to-all | bytes 12582912 | tf_op jit(solution)/shard_map/all_to_all | solution.py:39
  94.8 6.3 %convert_reduce_fusion = f32[2,384,512]{2,0,1:T(2,128)S(1)} fusion(bf16[2,8,384,512]{3,0,2,1:T(2,128)(2,1)S(1)} %bitcast.60), kind=kLoop, calls=%fused_computation.1 | loop fusion | flops 5898240 | bytes 7864320 | tf_op jit(solution)/shard_map/reduce_sum | solution.py:40
  101.1 0.0 copy-done.4
  101.1 0.0 copy-done.5
  101.1 0.0 copy-start.6
  101.1 2.7 %fusion.23 = (bf16[2,384,512]{2,1,0:T(8,128)(2,1)}, f32[2,384,512]{2,1,0:T(8,128)}, f32[2,384,512]{2,1,0:T(8,128)}) fusion(f32[2,384,512]{2,1,0:T(8,128)S(1)} %copy-done.4, f32[2,384,512]{2,0,1:T(2,128)S(1)} %convert_reduce_fusion, f32[2,384,512]{2,1,0:T(8,128)S(1)} %copy-done.5), kind=kLoop, calls=%fused_computation.41 | loop fusion | flops 3145728 | bytes 8650752 | tf_op jit(solution)/shard_map/convert_element_type | solution.py:42
  103.8 0.0 all-gather.3.cloned.1.call-update
  103.8 0.0 all-reduce.2.cloned.1.call-start
  103.8 0.0 copy-done.6
  103.9 19.8 %all-gather = bf16[512,768]{1,0:T(8,128)(2,1)S(1)} all-gather(bf16[128,768]{1,0:T(8,128)(2,1)S(1)} %copy-done.6), channel_id=2, replica_groups=mesh['replica'=8,'mp'=4] {'mp'}, dimensions={0}, use_global_device_ids=true | all-gather | bytes 983040 | tf_op jit(solution)/shard_map/all_gather | solution.py:37
  123.7 0.2 fusion.5
  123.9 0.0 copy-start.8
  124.0 0.0 copy-start.9
  124.0 0.3 fusion.16
  124.3 0.4 copy.48
  124.7 0.0 copy-done.7
  124.7 0.0 copy-start.2
  124.7 0.1 fusion.21
  124.8 0.1 copy-done.8
  124.9 0.1 copy-done.9
  124.9 0.2 fusion.14
  125.1 0.1 fusion.24
  125.2 23.5 %all-gather.3.cloned.1.call-done = bf16[2,3072,512]{2,1,0:T(8,128)(2,1)} async-done(((bf16[2,384,512]{2,1,0:T(8,128)(2,1)}), bf16[2,3072,512]{2,1,0:T(8,128)(2,1)}) %all-gather.3.cloned.1.call-update) | async-done | bytes 6291472 | tf_op jit(solution)/shard_map/all_gather | solution.py:42
  148.7 2.5 %fusion.11 = bf16[128,512]{1,0:T(8,128)(2,1)S(1)} fusion(bf16[128,3072]{0,1:T(8,128)(2,1)S(1)} %bitcast.64, bf16[2,3072,512]{2,1,0:T(8,128)(2,1)} %all-gather.3.cloned.1.call-done), kind=kOutput, calls=%fused_computation.26 | convolution fusion | flops 402784256 | bytes 4063232 | tf_op jit(solution)/shard_map/dot_general | solution.py:52
  151.2 0.0 copy-done.2
  151.2 0.1 copy.61
  151.3 0.2 convolution_convert_fusion.1
  151.6 4.0 %fusion.1 = bf16[128,3072]{1,0:T(8,128)(2,1)} fusion(bf16[128,512]{0,1:T(8,128)(2,1)S(1)} %bitcast.72, bf16[2,3072,512]{2,1,0:T(8,128)(2,1)} %all-gather.3.cloned.1.call-done), kind=kOutput, calls=%fused_computation.5 | convolution fusion | flops 403439616 | bytes 4063232 | tf_op jit(solution)/shard_map/dot_general | solution.py:62
  155.5 0.0 all-reduce.2.cloned.1.call-update
  155.5 0.1 convert_bitcast_fusion
  155.7 1.3 slice.30
  157.0 1.7 copy.49
  158.7 3.1 %copy.54 = f32[128,3072]{1,0:T(8,128)} copy(f32[128,3072]{0,1:T(8,128)} %bitcast.62) | data formatting | bytes 3145728 | tf_op jit(solution)/shard_map/convert_element_type | solution.py:47
  161.8 0.0 copy-done
  161.8 0.5 copy.55
  162.3 0.0 copy-start.1
  162.3 1.7 copy.56
  164.0 35.6 %all-reduce.2.cloned.1.call-done = bf16[128,3072]{1,0:T(8,128)(2,1)} async-done(((bf16[128,3072]{1,0:T(8,128)(2,1)}), bf16[128,3072]{1,0:T(8,128)(2,1)}) %all-reduce.2.cloned.1.call-update) | async-done | bytes 786448 | tf_op jit(solution)/shard_map/psum | solution.py:65
  199.6 3.2 %fusion.12 = bf16[128,512]{1,0:T(8,128)(2,1)S(1)} fusion(bf16[2,3072,512]{2,1,0:T(8,128)(2,1)} %all-gather.3.cloned.1.call-done, f32[1,3072]{1,0:T(1,128)S(1)} %bitcast.69, f32[127,3072]{1,0:T(8,128)} %copy.56, f32[128,3072]{1,0:T(8,128)S(1)} %copy-done.1, bf16[128,3072]{1,0:T(8,128)(2,1)} %all-reduce.2.cloned.1.call-done), kind=kOutput, calls=%fused_computation.27 | convolution fusion | flops 404750336 | bytes 7221248 | tf_op jit(solution)/shard_map/dot_general | solution.py:68
  202.8 0.0 copy-start.3
  202.8 0.1 copy.62
  202.9 0.2 convolution_convert_fusion
  203.2 0.8 copy-done.3
  203.9 5.0 %multiply_reduce_fusion = (f32[]{:T(128)}, f32[3072,512]{1,0:T(8,128)}) fusion(bf16[128,3072]{0,1:T(8,128)(2,1)S(1)} %bitcast.65, bf16[128,512]{0,1:T(8,128)(2,1)S(1)} %bitcast.66), kind=kOutput, calls=%fused_computation.3 | convolution fusion | flops 407371776 | bytes 7208964 | tf_op jit(solution)/shard_map/dot_general | solution.py:71
  208.9 10.6 %psum.15 = f32[]{:T(128)} all-reduce(f32[]{:T(128)} %get-tuple-element.6), channel_id=1, replica_groups=mesh['replica'=8,'mp'=4] {'mp'}, use_global_device_ids=true, to_apply=%region_6.7 | all-reduce | flops 1 | bytes 8 | tf_op jit(solution)/shard_map/psum | solution.py:77
  220.2 6.5 %fusion.2 = bf16[1,3072,512]{2,1,0:T(8,128)(2,1)} fusion(f32[]{:T(128)S(6)} %sqrt.3, f32[3072,512]{1,0:T(8,128)} %get-tuple-element.7, bf16[2,3072,512]{2,1,0:T(8,128)(2,1)} %all-gather.3.cloned.1.call-done), kind=kLoop, calls=%fused_computation.8 | loop fusion | flops 7864320 | bytes 12582916 | tf_op jit(solution)/shard_map/broadcast_in_dim | solution.py:80
  (7 shorter events, 0.0 us)
Async XLA Ops:
  7.2 141.5 %all-gather.3.cloned.1.call-start = ((), (), s32[]{:S(2)}) async-start(), calls=%async_computation.1 | async-start | bytes 7077888 | tf_op jit(solution)/shard_map/all_gather | solution.py:42
  94.8 6.3 %copy-start.4 = (f32[2,384,512]{2,1,0:T(8,128)S(1)}, f32[2,384,512]{2,1,0:T(8,128)}, u32[]{:S(2)}) copy-start(f32[2,384,512]{2,1,0:T(8,128)} %param.8) | copy-start | bytes 4718596
  94.8 6.3 %copy-start.5 = (f32[2,384,512]{2,1,0:T(8,128)S(1)}, f32[2,384,512]{2,1,0:T(8,128)}, u32[]{:S(2)}) copy-start(f32[2,384,512]{2,1,0:T(8,128)} %param.9) | copy-start | bytes 4718596
  101.1 2.8 %copy-start.6 = (bf16[128,768]{1,0:T(8,128)(2,1)S(1)}, bf16[128,768]{1,0:T(8,128)(2,1)}, u32[]{:S(2)}) copy-start(bf16[128,768]{1,0:T(8,128)(2,1)} %param.10) | copy-start | bytes 589828
  103.8 95.8 %all-reduce.2.cloned.1.call-start = ((), (), s32[]{:S(2)}) async-start(), calls=%async_computation.2 | async-start | bytes 1572864 | tf_op jit(solution)/shard_map/psum | solution.py:65
  123.9 0.7 copy-start.7
  123.9 0.9 copy-start.8
  124.0 1.0 copy-start.9
  124.7 26.5 %copy-start.2 = (bf16[128,4,768]{0,2,1:T(8,128)(2,1)}, bf16[128,4,768]{0,2,1:T(8,128)(2,1)S(1)}, u32[]{:S(2)}) copy-start(bf16[128,4,768]{0,2,1:T(8,128)(2,1)S(1)} %copy.48) | copy-start | bytes 2359300
  158.7 3.1 %copy-start = (f32[127,4,768]{2,0,1:T(8,128)S(1)}, f32[127,4,768]{2,0,1:T(8,128)}, u32[]{:S(2)}) copy-start(f32[127,4,768]{2,0,1:T(8,128)} %slice.30) | copy-start | bytes 4681732
  162.3 37.2 %copy-start.1 = (f32[128,3072]{1,0:T(8,128)S(1)}, f32[128,3072]{1,0:T(8,128)}, u32[]{:S(2)}) copy-start(f32[128,3072]{1,0:T(8,128)} %copy.54) | copy-start | bytes 4718596
  202.8 1.1 copy-start.3
Sparse Core Ops, SparseCore 0:
  103.9 44.7 all-gather.2
  155.7 43.8 all-reduce.1
